TPU v7x, 32 devices: a whole 2x2x4 slice. The times are simulated.
32 devices in a mesh: dp: 2 (over x), tp: 4 (over z), sp: 4 (over y, core).
Axes of the slice: x: 2, y: 2, z: 4, core: 2. Of those that a mesh axis runs over, the one named last changes fastest.
Arguments:
- x_tokens: bfloat16 [4096, 8192], P(('dp', 'sp'), 'tp'), parts along dimension 0
- doc_ids: int32 [4096], P(('dp', 'sp')), parts along dimension 0
- w_qkv: bfloat16 [8192, 24576], P('sp', 'tp')
- w_out: bfloat16 [8192, 8192], P('sp', 'tp')
Outputs:
- output: bfloat16 [4096, 8192], P(('dp', 'sp', 'tp')), parts along dimension 0
There are 2 independent parts. A program takes and returns all parts, laid end to end along the dimension named above; an argument that names none is the same for every part.
All inputs are finite; a program needn't handle non-finite values.
Results may differ from a plain program's by a relative error of at most 0.00292.
Values are sent between devices in bfloat16 or wider.
A program may use at most 1 GiB of HBM per device.

v0:
```python
import jax
import jax.numpy as jnp
from jax import lax
from jax.sharding import PartitionSpec as P

HEAD_DIM = 128
SOFTMAX_SCALE = HEAD_DIM ** -0.5


def solution(mesh):
    def device_block(x_block, doc_block, wqkv_block, wout_block):
        x_rows = lax.all_gather(x_block, "tp", axis=1, tiled=True)
        wqkv_cols = lax.all_gather(wqkv_block, "sp", axis=0, tiled=True)
        qkv_local = jnp.dot(x_rows, wqkv_cols, preferred_element_type=jnp.float32).astype(jnp.bfloat16)
        row_count = x_rows.shape[0]
        head_count = wqkv_cols.shape[1] // (3 * HEAD_DIM)
        qkv_local = qkv_local.reshape(row_count, head_count, 3, HEAD_DIM)
        query_loc = qkv_local[:, :, 0]
        kv_all = lax.all_gather(qkv_local[:, :, 1:], "sp", axis=0, tiled=True)
        doc_all = lax.all_gather(doc_block, "sp", axis=0, tiled=True)
        scores = jnp.einsum("qhd,khd->hqk", query_loc, kv_all[:, :, 0], preferred_element_type=jnp.float32) * SOFTMAX_SCALE
        same_doc = doc_block[:, None] == doc_all[None, :]
        scores = jnp.where(same_doc[None], scores, -jnp.inf)
        weights = jax.nn.softmax(scores, axis=-1).astype(jnp.bfloat16)
        context = jnp.einsum("hqk,khd->qhd", weights, kv_all[:, :, 1], preferred_element_type=jnp.float32).astype(jnp.bfloat16)
        context = context.reshape(row_count, head_count * HEAD_DIM)
        ctx_rows = lax.all_gather(context, "tp", axis=1, tiled=True)
        wout_cols = lax.all_gather(wout_block, "sp", axis=0, tiled=True)
        y_block = jnp.dot(ctx_rows, wout_cols, preferred_element_type=jnp.float32).astype(jnp.bfloat16)
        return lax.all_to_all(y_block, "tp", 0, 1, tiled=True)

    return jax.shard_map(
        device_block,
        mesh=mesh,
        in_specs=(P(("dp", "sp"), "tp"), P(("dp", "sp")), P("sp", "tp"), P("sp", "tp")),
        out_specs=P(("dp", "sp", "tp"), None),
        check_vma=False,
    )
```

profile of v0, /device:TPU:0, one launch (start us, length us, event | category | flops | bytes accessed | tf_op | source)
XLA Modules:
  0.0 1373.4 jit_solution(13565907103562229120)
XLA Ops:
  6.5 0.7 all-gather.7.cloned.1.call-update
  7.3 0.0 all-gather.9.cloned.1.call-start
  7.3 0.7 all-gather.9.cloned.1.call-update
  8.0 0.0 all-gather.11.cloned.1.call-start
  8.1 153.1 %all-gather.7.cloned.1.call-done = bf16[512,8192]{1,0:T(8,128)(2,1)} async-done(((bf16[512,2048]{1,0:T(8,128)(2,1)}), bf16[512,8192]{1,0:T(8,128)(2,1)}) %all-gather.7.cloned.1.call-update) | async-done | bytes 8388624 | tf_op jit(solution)/shard_map/all_gather | solution.py:12
  161.2 582.8 %all-gather.9.cloned.1.call-done = bf16[8192,6144]{1,0:T(8,128)(2,1)} async-done(((bf16[2048,6144]{1,0:T(8,128)(2,1)}), bf16[8192,6144]{1,0:T(8,128)(2,1)}) %all-gather.9.cloned.1.call-update) | async-done | bytes 100663312 | tf_op jit(solution)/shard_map/all_gather | solution.py:13
  744.0 61.2 %convolution_convert_fusion = bf16[512,6144]{1,0:T(8,128)(2,1)} fusion(bf16[512,8192]{1,0:T(8,128)(2,1)} %all-gather.7.cloned.1.call-done, bf16[8192,6144]{1,0:T(8,128)(2,1)} %all-gather.9.cloned.1.call-done), kind=kOutput, calls=%fused_computation.9 | convolution fusion | flops 51542753280 | bytes 115343360 | tf_op jit(solution)/shard_map/dot_general | solution.py:14
  805.1 8.6 copy.14
  813.8 4.6 slice.16
  818.4 6.2 copy.20
  824.6 0.0 all-gather.15.cloned.1.call-start
  824.6 0.5 all-gather.15.cloned.1.call-update
  825.2 0.0 all-gather.13.cloned.1.call-start
  825.2 5.2 all-gather
  830.4 0.7 broadcast_compare_fusion
  831.0 100.6 %all-gather.11.cloned.1.call-done = bf16[2048,16,2,128]{3,0,1,2:T(8,128)(2,1)} async-done(((bf16[512,16,2,128]{3,0,1,2:T(8,128)(2,1)}), bf16[2048,16,2,128]{3,0,1,2:T(8,128)(2,1)}) %all-gather.11.cloned.1.call-update) | async-done | bytes 16777232 | tf_op jit(solution)/shard_map/all_gather | solution.py:19
  931.7 27.1 %fusion.6 = f32[16,512,2048]{2,1,0:T(8,128)} fusion(bf16[2048,16,2,128]{3,0,1,2:T(8,128)(2,1)} %all-gather.11.cloned.1.call-done, bf16[512,16,3,128]{0,3,2,1:T(8,128)(2,1)} %bitcast.27), kind=kOutput, calls=%fused_computation.11 | convolution fusion | flops 4294967296 | bytes 77594624 | tf_op jit(solution)/shard_map/qhd,khd->hqk/dot_general | solution.py:21
  958.8 68.7 %fusion.10 = (f32[16,512]{1,0:T(8,128)S(1)}, f32[16,512,2048]{2,1,0:T(8,128)}) fusion(f32[16,512,2048]{2,1,0:T(8,128)} %fusion.6, pred[512,2048]{1,0:T(8,128)(4,1)S(1)} %broadcast_compare_fusion), kind=kOutput, calls=%fused_computation.19 | output fusion | flops 100665344 | bytes 135299072 | tf_op jit(solution)/shard_map/sub | solution.py:24
  1027.4 27.2 %fusion.7 = bf16[16,128,512]{2,1,0:T(8,128)(2,1)} fusion(f32[16,512,2048]{2,1,0:T(8,128)} %get-tuple-element.6, f32[16,512]{1,0:T(8,128)S(1)} %get-tuple-element.5, bf16[2048,16,2,128]{3,0,1,2:T(8,128)(2,1)} %all-gather.11.cloned.1.call-done), kind=kOutput, calls=%fused_computation.16 | convolution fusion | flops 4329570304 | bytes 77627392 | tf_op jit(solution)/shard_map/hqk,khd->qhd/dot_general | solution.py:25
  1054.7 80.6 %all-gather.15.cloned.1.call-done = bf16[8192,2048]{1,0:T(8,128)(2,1)} async-done(((bf16[2048,2048]{1,0:T(8,128)(2,1)}), bf16[8192,2048]{1,0:T(8,128)(2,1)}) %all-gather.15.cloned.1.call-update) | async-done | bytes 33554448 | tf_op jit(solution)/shard_map/all_gather | solution.py:28
  1135.3 150.9 %all-gather.13.cloned.1.call-done = bf16[512,8192]{0,1:T(8,128)(2,1)} async-done(((bf16[512,2048]{0,1:T(8,128)(2,1)}), bf16[512,8192]{0,1:T(8,128)(2,1)}) %all-gather.13.cloned.1.call-update) | async-done | bytes 8388624 | tf_op jit(solution)/shard_map/all_gather | solution.py:27
  1286.2 23.9 %convolution_convert_fusion.1 = bf16[512,2048]{1,0:T(8,128)(2,1)S(1)} fusion(bf16[512,8192]{0,1:T(8,128)(2,1)} %all-gather.13.cloned.1.call-done, bf16[8192,2048]{1,0:T(8,128)(2,1)} %all-gather.15.cloned.1.call-done), kind=kOutput, calls=%fused_computation.13 | convolution fusion | flops 17180917760 | bytes 44040192 | tf_op jit(solution)/shard_map/dot_general | solution.py:29
  1310.1 55.3 %all_to_all.19 = bf16[4,128,2048]{2,1,0:T(8,128)(2,1)S(1)} all-to-all(bf16[4,128,2048]{2,1,0:T(8,128)(2,1)S(1)} %bitcast.30), channel_id=1, replica_groups=mesh['dp'=2,'tp'=4,'sp'=4] {'tp'}, dimensions={0} | all-to-all | bytes 4194304 | tf_op jit(solution)/shard_map/all_to_all | solution.py:30
  1365.4 1.5 copy.22
  (5 shorter events, 0.0 us)
Async XLA Ops:
  6.5 154.6 %all-gather.7.cloned.1.call-start = ((), (), s32[]{:S(2)}) async-start(), calls=%async_computation.1 | async-start | bytes 10485760 | tf_op jit(solution)/shard_map/all_gather | solution.py:12
  7.3 736.7 %all-gather.9.cloned.1.call-start = ((), (), s32[]{:S(2)}) async-start(), calls=%async_computation.2 | async-start | bytes 125829120 | tf_op jit(solution)/shard_map/all_gather | solution.py:13
  8.0 923.7 %all-gather.11.cloned.1.call-start = ((), (), s32[]{:S(2)}) async-start(), calls=%async_computation.3 | async-start | bytes 20971520 | tf_op jit(solution)/shard_map/all_gather | solution.py:19
  813.8 11.4 copy-start
  824.6 310.7 %all-gather.15.cloned.1.call-start = ((), (), s32[]{:S(2)}) async-start(), calls=%async_computation.5 | async-start | bytes 41943040 | tf_op jit(solution)/shard_map/all_gather | solution.py:28
  825.2 461.1 %all-gather.13.cloned.1.call-start = ((), (), s32[]{:S(2)}) async-start(), calls=%async_computation.4 | async-start | bytes 10485760 | tf_op jit(solution)/shard_map/all_gather | solution.py:27
Sparse Core Ops, SparseCore 0:
  8.9 152.2 all-gather.6
  162.7 581.1 all-gather.8
  824.7 106.9 all-gather.10
  933.1 202.1 all-gather.14
  1136.7 149.4 all-gather.12
where the time goes:
time: 1370 us
  waiting for transfers between devices  1070 us (78%)
  matrix products  139 us (10%)
  other arithmetic  69.3 us (5%)
  blocking collectives  60.5 us (4%)
  local copies, waits for them, and re-layouts  20.9 us (2%)
    all_gather x1, waiting for transfers between devices, device_block(): wqkv_cols = lax.all_gather(wqkv_block, 'sp', axis=0, tiled=True)  583 us
    all_gather x1, waiting for transfers between devices, device_block(): x_rows = lax.all_gather(x_block, 'tp', axis=1, tiled=True)  153 us
    all_gather x1, waiting for transfers between devices, device_block(): ctx_rows = lax.all_gather(context, 'tp', axis=1, tiled=True)  151 us
    all_gather x1, waiting for transfers between devices, device_block(): kv_all = lax.all_gather(qkv_local[:, :, 1:], 'sp', axis=0, tiled=True)  101 us
    all_gather x1, waiting for transfers between devices, device_block(): wout_cols = lax.all_gather(wout_block, 'sp', axis=0, tiled=True)  80.6 us
    sub x1, other arithmetic, device_block(): weights = jax.nn.softmax(scores, axis=-1).astype(jnp.bfloat16)  68.7 us
    dot_general x1, matrix products, device_block(): jnp.dot(x_rows, wqkv_cols, preferred_element_type=jnp.float32)  61.2 us
    all_to_all x1, blocking collectives, device_block(): return lax.all_to_all(y_block, 'tp', 0, 1, tiled=True)  55.3 us
  transfers between devices with their start and end apart: 5, of which 5 were waited for; matrix products, arithmetic and copies ran while one was open for 9% of the time, Pallas kernels for 0%

commit v1 on v0

v1 whole, which is shorter than its diff:
```python
import functools

import jax
import jax.numpy as jnp
from jax import lax
from jax.experimental import pallas as pl
from jax.experimental.pallas import tpu as pltpu
from jax.sharding import PartitionSpec as P

HEAD_DIM = 128
SOFTMAX_SCALE = HEAD_DIM ** -0.5
MESH = pl.DeviceIdType.MESH
VMEM_LIMIT = 67_000_000

PIECES = 4
FIRST = 2
WCHUNKS = 4


def sp_peers(sp):
    core = lax.rem(sp, 2)
    return sp + 1 - 2 * core, lax.rem(sp + 2, 4), 3 - sp


def send(src, dst, ssem, rsem, **device):
    copy = pltpu.make_async_remote_copy(
        src_ref=src, dst_ref=dst, send_sem=ssem, recv_sem=rsem, device_id=device, device_id_type=MESH
    )
    copy.start()


def wait_bytes(ref, sem):
    pltpu.make_async_copy(ref, ref, sem).wait()


def enter(peers):
    barrier = pltpu.get_barrier_semaphore()
    for peer in peers:
        pl.semaphore_signal(barrier, inc=1, device_id=peer, device_id_type=MESH)
    pl.semaphore_wait(barrier, len(peers))


def aligned(index, size):
    return pl.ds(pl.multiple_of(index * size, size), size)


def qkv_kernel(x_ref, seg_ref, w_ref, qkv_ref, segs_ref, xf, wf, stage,
               loc, ys, yr, zs, zr, xs, xr, ds, dr, gs, gr, outs):
    dp, z, sp = lax.axis_index("dp"), lax.axis_index("tp"), lax.axis_index("sp")
    cp, yp, ycp = sp_peers(sp)
    xp = 1 - dp
    rows, cols = x_ref.shape
    depth = w_ref.shape[0]
    group = w_ref.shape[1] // 4
    piece = rows // PIECES
    late = PIECES - FIRST
    items = PIECES + late
    half = depth // 2
    chunk = half // WCHUNKS

    enter([{"sp": cp}, {"sp": yp}, {"sp": ycp}, {"dp": xp}, {"tp": lax.rem(z + 1, 4)}, {"tp": lax.rem(z + 3, 4)}])

    def item_start(i, own, across):
        return own * PIECES + i if i < PIECES else across * PIECES + FIRST + i - PIECES

    def item_rows(i):
        return aligned(item_start(i, sp, yp), piece)

    def block(i, k):
        return xf.at[item_rows(i), aligned(k, cols)]

    def to_core(i, k):
        send(block(i, k), block(i, k), ds.at[i], dr.at[i], sp=cp)

    def z_send(i, d, s):
        if d == 0:
            @pl.when((z <= 2) & (z >= s - 1))
            def _():
                k = z - (s - 1)
                send(block(i, k), block(i, k), zs.at[i, d, s - 1], zr.at[i, d, s - 1], tp=z + 1)
        else:
            @pl.when((z >= 1) & (z + s - 1 <= 3))
            def _():
                k = z + (s - 1)
                send(block(i, k), block(i, k), zs.at[i, d, s - 1], zr.at[i, d, s - 1], tp=z - 1)

    def z_recv(i, s):
        @pl.when(z >= s)
        def _():
            wait_bytes(block(i, z - s), zr.at[i, 0, s - 1])
            if s < 3:
                z_send(i, 0, s + 1)
            to_core(i, z - s)

        @pl.when(z + s <= 3)
        def _():
            wait_bytes(block(i, z + s), zr.at[i, 1, s - 1])
            if s < 3:
                z_send(i, 1, s + 1)
            to_core(i, z + s)

    def w_rows(quarter, x_half, c):
        return aligned((quarter * 2 + x_half) * WCHUNKS + c, chunk)

    def w_recv(n):
        source = (yp, ycp)[n % 2]
        ref = wf.at[w_rows(source, dp, n // 2), :]
        wait_bytes(ref, yr.at[late + n])
        send(ref, ref, xs.at[n], xr.at[n % 2], dp=xp)

    x_own = pltpu.make_async_copy(x_ref, xf.at[aligned(sp, rows), aligned(z, cols)], loc.at[0])
    x_own.start()
    w_own = pltpu.make_async_copy(w_ref.at[:, aligned(sp, group)], wf.at[aligned(sp, depth), :], loc.at[1])
    w_own.start()
    seg_own = pltpu.make_async_copy(seg_ref, segs_ref.at[sp], loc.at[2])
    seg_own.start()
    for n, peer in enumerate((cp, yp, ycp)):
        send(seg_ref, segs_ref.at[sp], gs.at[n], gr.at[n], sp=peer)
    x_own.wait()
    for j in range(late):
        i = FIRST + j
        send(block(i, z), block(i, z), ys.at[j], yr.at[j], sp=yp)
    for n in range(2 * WCHUNKS):
        target = (yp, ycp)[n % 2]
        local = aligned(dp * WCHUNKS + n // 2, chunk)
        send(w_ref.at[local, aligned(target, group)], wf.at[w_rows(sp, dp, n // 2), :],
             ys.at[late + n], yr.at[late + n], sp=target)
    for i in range(PIECES):
        z_send(i, 0, 1)
        z_send(i, 1, 1)
    for i in range(PIECES):
        to_core(i, z)
    send(w_ref.at[:, aligned(cp, group)], wf.at[aligned(sp, depth), :], ds.at[items + FIRST], dr.at[items + FIRST], sp=cp)

    def y_recv(j):
        i = PIECES + j
        wait_bytes(block(i, z), yr.at[j])
        z_send(i, 0, 1)
        z_send(i, 1, 1)
        to_core(i, z)

    def q_send(i):
        ref = xf.at[item_rows(i), :]
        send(ref, ref, ys.at[late + 2 * WCHUNKS + i], yr.at[late + 2 * WCHUNKS + i], sp=yp)

    def q_rows(i, owner):
        return aligned(owner * PIECES + i, piece)

    def q_recv(i):
        ref = xf.at[q_rows(i, yp), :]
        wait_bytes(ref, yr.at[late + 2 * WCHUNKS + i])
        send(ref, ref, ds.at[items + i], dr.at[items + i], sp=cp)

    z_recv(0, 1)
    for j in range(late):
        y_recv(j)
    z_recv(1, 1)
    z_recv(2, 1)
    w_recv(0)
    z_recv(3, 1)
    w_recv(1)
    for i in range(PIECES, items):
        z_recv(i, 1)
    w_recv(2)
    z_recv(0, 2)
    z_recv(1, 2)
    w_recv(3)
    z_recv(2, 2)
    w_recv(4)
    z_recv(3, 2)
    w_recv(5)
    for i in range(PIECES, items):
        z_recv(i, 2)
    w_recv(6)
    for i in range(FIRST):
        z_recv(i, 3)
        q_send(i)
    w_recv(7)

    tile = 512 if group % 512 == 0 else group
    count = [0]

    def matmul(start, size):
        slot = count[0] % 2
        span = aligned(start, size)
        if count[0] >= 2:
            wait_bytes(stage.at[slot, pl.ds(0, sizes[count[0] - 2]), :], outs.at[slot])
        sizes.append(size)

        def step(n, carry):
            at = aligned(n, tile)
            stage[slot, 0:size, at] = jnp.dot(
                xf[span, :], wf[:, at], preferred_element_type=jnp.float32).astype(jnp.bfloat16)
            return carry

        lax.fori_loop(0, group // tile, step, 0)
        pltpu.make_async_copy(stage.at[slot, pl.ds(0, size), :], qkv_ref.at[span, :], outs.at[slot]).start()
        count[0] += 1

    sizes = []

    def core_rows(i):
        if i < items:
            return aligned(item_start(i, cp, ycp), piece)
        return q_rows(i - items, ycp)

    def from_core(i):
        wait_bytes(xf.at[core_rows(i), :], dr.at[i])

    w_own.wait()
    wait_bytes(wf.at[aligned(cp, depth), :], dr.at[items + FIRST])
    for n, source in enumerate((yp, ycp)):
        wait_bytes(wf.at[aligned(source * 2 + xp, half), :], xr.at[n])

    unit = FIRST * piece
    assert FIRST == late
    matmul(sp * 2, unit)
    for i in range(FIRST):
        from_core(i)
    for i in range(FIRST, PIECES):
        z_recv(i, 3)
    matmul(cp * 2, unit)
    for i in range(PIECES, items):
        z_recv(i, 3)
    matmul(sp * 2 + 1, unit)
    q_recv(0)
    for i in range(FIRST, PIECES):
        from_core(i)
    matmul(cp * 2 + 1, unit)
    for i in range(PIECES, items):
        from_core(i)
    matmul(yp * 2 + 1, unit)
    matmul(ycp * 2 + 1, unit)
    for i in range(1, FIRST):
        q_recv(i)
    matmul(yp * 2, unit)
    for i in range(FIRST):
        from_core(items + i)
    matmul(ycp * 2, unit)

    for slot in range(2):
        wait_bytes(stage.at[slot, pl.ds(0, unit), :], outs.at[slot])
    seg_own.wait()
    for n, peer in enumerate((cp, yp, ycp)):
        wait_bytes(seg_ref, gs.at[n])
        wait_bytes(segs_ref.at[peer], gr.at[n])
    for j in range(late):
        wait_bytes(block(FIRST + j, z), ys.at[j])
    for n in range(2 * WCHUNKS):
        ref = wf.at[pl.ds(0, chunk), :]
        wait_bytes(ref, ys.at[late + n])
        wait_bytes(ref, xs.at[n])
    for i in range(FIRST):
        wait_bytes(xf.at[item_rows(i), :], ys.at[late + 2 * WCHUNKS + i])
        wait_bytes(xf.at[q_rows(i, yp), :], ds.at[items + i])
    for i in range(items):
        wait_bytes(xf.at[item_rows(i), :], ds.at[i])
        for s in range(1, 4):
            @pl.when((z <= 2) & (z >= s - 1))
            def _():
                wait_bytes(block(i, z), zs.at[i, 0, s - 1])

            @pl.when((z >= 1) & (z + s - 1 <= 3))
            def _():
                wait_bytes(block(i, z), zs.at[i, 1, s - 1])
    wait_bytes(wf.at[aligned(sp, depth), :], ds.at[items + FIRST])


def gather_qkv(x, seg, w):
    rows, cols = x.shape
    depth, width = w.shape
    group = width // 4
    late = PIECES - FIRST
    items = PIECES + late
    crossings = late + 2 * WCHUNKS + FIRST
    dma = pltpu.SemaphoreType.DMA
    any_space = pl.BlockSpec(memory_space=pl.ANY)
    return pl.pallas_call(
        qkv_kernel,
        out_shape=(
            jax.ShapeDtypeStruct((4 * rows, group), jnp.bfloat16),
            jax.ShapeDtypeStruct((4,) + seg.shape, jnp.int32),
        ),
        in_specs=[any_space] * 3,
        out_specs=(any_space, any_space),
        scratch_shapes=[
            pltpu.VMEM((4 * rows, 4 * cols), jnp.bfloat16),
            pltpu.VMEM((4 * depth, group), jnp.bfloat16),
            pltpu.VMEM((2, FIRST * rows // PIECES, group), jnp.bfloat16),
            dma((3,)),
            dma((crossings,)),
            dma((crossings,)),
            dma((items, 2, 3)),
            dma((items, 2, 3)),
            dma((2 * WCHUNKS,)),
            dma((2,)),
            dma((items + FIRST + 1,)),
            dma((items + FIRST + 1,)),
            dma((3,)),
            dma((3,)),
            dma((2,)),
        ],
        compiler_params=pltpu.CompilerParams(collective_id=0, has_side_effects=True, vmem_limit_bytes=VMEM_LIMIT),
        name="gather_qkv",
    )(x, seg, w)


def attention_kernel(q_ref, k_ref, v_ref, segq_ref, segk_ref, o_ref):
    scores = lax.dot_general(q_ref[...], k_ref[...], (((1,), (1,)), ((), ())), preferred_element_type=jnp.float32)
    scores = jnp.where(segq_ref[...] == segk_ref[...], scores * SOFTMAX_SCALE, -jnp.inf)
    top = jnp.max(scores, axis=1, keepdims=True)
    weights = jnp.exp(scores - top)
    weights = (weights / jnp.sum(weights, axis=1, keepdims=True)).astype(jnp.bfloat16)
    o_ref[...] = jnp.dot(weights, v_ref[...], preferred_element_type=jnp.float32).astype(jnp.bfloat16)


def attention(qkv, segs):
    tokens, width = qkv.shape
    heads = width // (3 * HEAD_DIM)
    block = min(256, tokens)
    return pl.pallas_call(
        attention_kernel,
        out_shape=jax.ShapeDtypeStruct((tokens, heads * HEAD_DIM), jnp.bfloat16),
        grid=(heads, tokens // block),
        in_specs=[
            pl.BlockSpec((block, HEAD_DIM), lambda h, i: (i, 3 * h)),
            pl.BlockSpec((tokens, HEAD_DIM), lambda h, i: (0, 3 * h + 1)),
            pl.BlockSpec((tokens, HEAD_DIM), lambda h, i: (0, 3 * h + 2)),
            pl.BlockSpec((block, 1), lambda h, i: (i, 0)),
            pl.BlockSpec((1, tokens), lambda h, i: (0, 0)),
        ],
        out_specs=pl.BlockSpec((block, HEAD_DIM), lambda h, i: (i, h)),
        name="attention",
    )(qkv, qkv, qkv, segs.reshape(tokens, 1), segs.reshape(1, tokens))


def out_kernel(o_ref, w_ref, y_ref, of, wf, acc, stage,
               loc, os, orr, zs, zr, ys, yr, xs, xr, ds, dr, fs, fr, outl):
    dp, z, sp = lax.axis_index("dp"), lax.axis_index("tp"), lax.axis_index("sp")
    cp, yp, ycp = sp_peers(sp)
    xp = 1 - dp
    y = sp // 2
    tokens, width = o_ref.shape
    rows = tokens // 4
    depth, cols = w_ref.shape
    half = depth // 2
    chunk = half // WCHUNKS
    sources = (sp, cp, yp, ycp)

    enter([{"sp": cp}, {"sp": yp}, {"sp": ycp}, {"dp": xp}] + [{"tp": lax.rem(z + r, 4)} for r in (1, 2, 3)])

    def block(j, k):
        return of.at[:, aligned(k * 4 + sources[j], width)]

    def z_send(j, d, s):
        if d == 0:
            @pl.when((z <= 2) & (z >= s - 1))
            def _():
                k = z - (s - 1)
                send(block(j, k), block(j, k), zs.at[j, d, s - 1], zr.at[j, d, s - 1], tp=z + 1)
        else:
            @pl.when((z >= 1) & (z + s - 1 <= 3))
            def _():
                k = z + (s - 1)
                send(block(j, k), block(j, k), zs.at[j, d, s - 1], zr.at[j, d, s - 1], tp=z - 1)

    def z_recv(j, s):
        @pl.when(z >= s)
        def _():
            wait_bytes(block(j, z - s), zr.at[j, 0, s - 1])
            if s < 3:
                z_send(j, 0, s + 1)

        @pl.when(z + s <= 3)
        def _():
            wait_bytes(block(j, z + s), zr.at[j, 1, s - 1])
            if s < 3:
                z_send(j, 1, s + 1)

    def w_rows(quarter, x_half, c):
        return aligned((quarter * 2 + x_half) * WCHUNKS + c, chunk)

    def w_recv(n):
        ref = wf.at[w_rows(yp, dp, n), :]
        wait_bytes(ref, yr.at[n])
        send(ref, ref, xs.at[n], xr.at[n], dp=xp)
        send(ref, ref, ds.at[1], dr.at[1], sp=cp)

    def x_recv(n):
        ref = wf.at[w_rows(yp, xp, n), :]
        wait_bytes(ref, xr.at[n])
        send(ref, ref, ds.at[2], dr.at[2], sp=cp)

    o_own = pltpu.make_async_copy(o_ref.at[aligned(sp, rows), :], block(0, z), loc.at[0])
    o_own.start()
    for n, peer in enumerate((cp, yp, ycp)):
        send(o_ref.at[aligned(peer, rows), :], block(0, z), os.at[n], orr.at[n], sp=peer)
    for n in range(WCHUNKS):
        send(w_ref.at[aligned(dp * WCHUNKS + n, chunk), :], wf.at[w_rows(sp, dp, n), :], ys.at[n], yr.at[n], sp=yp)
    o_own.wait()
    z_send(0, 0, 1)
    z_send(0, 1, 1)
    w_own = pltpu.make_async_copy(w_ref, wf.at[aligned(sp, depth), :], loc.at[1])
    w_own.start()
    for n in range(3):
        wait_bytes(block(1 + n, z), orr.at[n])
        z_send(1 + n, 0, 1)
        z_send(1 + n, 1, 1)
        if n == 0:
            send(w_ref, wf.at[aligned(sp, depth), :], ds.at[0], dr.at[0], sp=cp)
            acc[...] = jnp.zeros_like(acc)
            z_recv(0, 1)
    z_recv(1, 1)
    z_recv(2, 1)
    w_recv(0)
    z_recv(3, 1)
    z_recv(0, 2)
    w_recv(1)
    z_recv(1, 2)
    x_recv(0)
    z_recv(2, 2)
    w_recv(2)
    z_recv(3, 2)
    x_recv(1)

    tile = min(512, cols)
    tiles = cols // tile

    def add_block(k):
        def step(n, carry):
            at = aligned(n, tile)
            acc[:, at] += jnp.dot(of[:, aligned(k, depth)], wf[aligned(k, depth), at],
                                  preferred_element_type=jnp.float32)
            return carry

        lax.fori_loop(0, tiles, step, 0)

    def near_blocks(when):
        for b in range(2):
            k = 2 * y + b

            @pl.when(when(k - z))
            def _():
                add_block(k)

    w_own.wait()
    wait_bytes(wf.at[aligned(cp, depth), :], dr.at[0])
    z_recv(0, 3)
    near_blocks(lambda gap: (gap <= 2) & (gap >= -2))
    w_recv(3)
    z_recv(1, 3)
    x_recv(2)
    z_recv(2, 3)
    x_recv(3)
    z_recv(3, 3)
    near_blocks(lambda gap: (gap > 2) | (gap < -2))
    for n in range(2):
        wait_bytes(wf.at[aligned(ycp * 2 + (dp, xp)[n], half), :], dr.at[1 + n])

    far = aligned(1 - y, 2 * depth)
    part = rows // 4
    for n in range(tiles):
        at = pl.ds(n * tile, tile)
        stage[:, at] = (acc[:, at] + jnp.dot(of[:, far], wf[far, at], preferred_element_type=jnp.float32)
                        ).astype(jnp.bfloat16)
        there = pl.ds(pl.multiple_of(z * cols + n * tile, tile), tile)
        for r in (2, 1, 3):
            to = lax.rem(z + r, 4)
            send(stage.at[aligned(to, part), at], y_ref.at[:, there], fs.at[r - 1], fr.at[r - 1], tp=to)
        pltpu.make_async_copy(stage.at[aligned(z, part), at], y_ref.at[:, there], outl.at[0]).start()

    for r in (1, 2, 3):
        source = lax.rem(z + 4 - r, 4)
        wait_bytes(y_ref.at[:, aligned(source, cols)], fr.at[r - 1])
        wait_bytes(stage.at[aligned(z, part), :], fs.at[r - 1])
    wait_bytes(y_ref.at[:, aligned(z, cols)], outl.at[0])
    for n, peer in enumerate((cp, yp, ycp)):
        wait_bytes(block(0, z), os.at[n])
    for n in range(WCHUNKS):
        ref = wf.at[pl.ds(0, chunk), :]
        wait_bytes(ref, ys.at[n])
        wait_bytes(ref, xs.at[n])
    wait_bytes(wf.at[aligned(sp, depth), :], ds.at[0])
    for n in range(2):
        wait_bytes(wf.at[aligned(yp * 2 + (dp, xp)[n], half), :], ds.at[1 + n])
    for j in range(4):
        for s in range(1, 4):
            @pl.when((z <= 2) & (z >= s - 1))
            def _():
                wait_bytes(block(j, z), zs.at[j, 0, s - 1])

            @pl.when((z >= 1) & (z + s - 1 <= 3))
            def _():
                wait_bytes(block(j, z), zs.at[j, 1, s - 1])


def project_out(o, w):
    tokens, width = o.shape
    rows = tokens // 4
    depth, cols = w.shape
    dma = pltpu.SemaphoreType.DMA
    any_space = pl.BlockSpec(memory_space=pl.ANY)
    return pl.pallas_call(
        out_kernel,
        out_shape=jax.ShapeDtypeStruct((rows // 4, 4 * cols), jnp.bfloat16),
        in_specs=[any_space] * 2,
        out_specs=any_space,
        scratch_shapes=[
            pltpu.VMEM((rows, 4 * depth), jnp.bfloat16),
            pltpu.VMEM((4 * depth, cols), jnp.bfloat16),
            pltpu.VMEM((rows, cols), jnp.float32),
            pltpu.VMEM((rows, cols), jnp.bfloat16),
            dma((2,)),
            dma((3,)),
            dma((3,)),
            dma((4, 2, 3)),
            dma((4, 2, 3)),
            dma((WCHUNKS,)),
            dma((WCHUNKS,)),
            dma((WCHUNKS,)),
            dma((WCHUNKS,)),
            dma((3,)),
            dma((3,)),
            dma((3,)),
            dma((3,)),
            dma((1,)),
        ],
        compiler_params=pltpu.CompilerParams(collective_id=1, has_side_effects=True, vmem_limit_bytes=VMEM_LIMIT),
        name="project_out",
    )(o, w)


def solution(mesh):
    shape = dict(mesh.shape)
    assert shape == {"dp": 2, "tp": 4, "sp": 4}

    def device_block(x_block, doc_block, wqkv_block, wout_block):
        qkv, segs = gather_qkv(x_block, doc_block.reshape(-1, HEAD_DIM), wqkv_block)
        return project_out(attention(qkv, segs), wout_block)

    return jax.shard_map(
        device_block,
        mesh=mesh,
        in_specs=(P(("dp", "sp"), "tp"), P(("dp", "sp")), P("sp", "tp"), P("sp", "tp")),
        out_specs=P(("dp", "sp", "tp"), None),
        check_vma=False,
    )
```

time: 1370 us -> 511 us (0.37)
  waiting for transfers between devices: 1070 us -> 0 us
  Pallas kernels: 0 us -> 503 us
  matrix products: 139 us -> 0 us
  other arithmetic: 69.3 us -> 0 us
  blocking collectives: 60.5 us -> 0 us
  local copies, waits for them, and re-layouts: 20.9 us -> 5.16 us
    all_gather x5 -> x0, waiting for transfers between devices: 1070 us -> none  [the longest x1 583 us: device_block(): wqkv_cols = lax.all_gather(wqkv_block, 'sp', axis=0, tiled=True)]
    pallas_call x0 -> x3, Pallas kernels: none -> 503 us  [the longest x1 272 us: gather_qkv(): pl.pallas_call(qkv_kernel, out_shape=(jax.ShapeDtypeStruct((4 * rows, gro...]
    dot_general x4 -> x0, matrix products: 139 us -> none  [the longest x1 61.2 us: device_block(): jnp.dot(x_rows, wqkv_cols, preferred_element_type=jnp.float32)]
    sub x1 -> x0, other arithmetic: 68.7 us -> none  [device_block(): weights = jax.nn.softmax(scores, axis=-1).astype(jnp.bfloat16)]
    all_to_all x1 -> x0, blocking collectives: 55.3 us -> none  [device_block(): return lax.all_to_all(y_block, 'tp', 0, 1, tiled=True)]
  transfers between devices with their start and end apart: 5 -> 0, of which waited for: 5 -> 0; matrix products, arithmetic and copies ran while one was open for 9% -> 0% of each run, Pallas kernels for 0% -> 0%
where the time goes in v1:
time: 511 us; the launch traced here: 508 us
  Pallas kernels  503 us (98%)
  local copies, waits for them, and re-layouts  5.16 us (1%)
    pallas_call x1, Pallas kernels, gather_qkv(): pl.pallas_call(qkv_kernel, out_shape=(jax.ShapeDtypeStruct((4 * rows, gro...  272 us
    pallas_call x1, Pallas kernels, project_out(): pl.pallas_call(out_kernel, out_shape=jax.ShapeDtypeStruct((rows // 4, 4 *...  185 us
    pallas_call x1, Pallas kernels, attention(): pl.pallas_call(attention_kernel, out_shape=jax.ShapeDtypeStruct((tokens,...  45.5 us

profile of v1, /device:TPU:0, one launch (start us, length us, event | category | flops | bytes accessed | tf_op | source)
XLA Modules:
  0.0 507.8 jit_solution(4731786722999102000)
XLA Ops:
  0.0 272.1 %gather_qkv.1 = (bf16[2048,1536]{1,0:T(8,128)(2,1)}, s32[4,4,128]{2,1,0:T(4,128)}) custom-call(bf16[512,2048]{1,0:T(8,128)(2,1)} %x_ref.1, s32[4,128]{1,0:T(4,128)} %bitcast.5, bf16[2048,6144]{1,0:T(8,128)(2,1)} %w_ref.2), custom_call_target="tpu_custom_call" | custom-call | tf_op jit(solution)/shard_map/gather_qkv/pallas_call | solution.py:278
  272.1 2.1 copy.5.segq_ref
  274.2 45.5 %attention.1.o_ref = bf16[2048,512]{1,0:T(8,128)(2,1)} custom-call(bf16[2048,1536]{1,0:T(8,128)(2,1)} %get-tuple-element.7.q_ref.k_ref.v_ref, bf16[2048,1536]{1,0:T(8,128)(2,1)} %get-tuple-element.7.q_ref.k_ref.v_ref, bf16[2048,1536]{1,0:T(8,128)(2,1)} %get-tuple-element.7.q_ref.k_ref.v_ref, s32[2048,1]{1,0:T(8,128)} %copy.5.segq_ref, s32[1,2048]{1,0:T(1,128)} %bitcast.4), custom_call_target="tpu_custom_call" | custom-call | tf_op jit(solution)/shard_map/attention/pallas_call | solution.py:321
  319.7 185.0 %project_out.1 = bf16[128,8192]{1,0:T(8,128)(2,1)} custom-call(bf16[2048,512]{1,0:T(8,128)(2,1)} %attention.1.o_ref, bf16[2048,2048]{1,0:T(8,128)(2,1)} %w_ref.3), custom_call_target="tpu_custom_call" | custom-call | tf_op jit(solution)/shard_map/project_out/pallas_call | solution.py:503
  504.7 3.1 copy.7

commit v2 on v1

--- a/solution.py
+++ b/solution.py
@@ -9,12 +9,15 @@
 
 HEAD_DIM = 128
 SOFTMAX_SCALE = HEAD_DIM ** -0.5
+LOG2_E = 1.4426950408889634
 MESH = pl.DeviceIdType.MESH
 VMEM_LIMIT = 67_000_000
 
 PIECES = 4
 FIRST = 2
-WCHUNKS = 4
+SHARES = (3, 3, 5, 5)
+QKV_CHUNKS = 8
+OUT_CHUNKS = 4
 
 
 def sp_peers(sp):
@@ -52,19 +55,24 @@
     rows, cols = x_ref.shape
     depth = w_ref.shape[0]
     group = w_ref.shape[1] // 4
-    piece = rows // PIECES
+    unit = rows // 16
+    sizes = [share * unit for share in SHARES]
+    offsets = [sum(sizes[:i]) for i in range(PIECES)]
     late = PIECES - FIRST
     items = PIECES + late
     half = depth // 2
-    chunk = half // WCHUNKS
+    chunk = half // QKV_CHUNKS
 
     enter([{"sp": cp}, {"sp": yp}, {"sp": ycp}, {"dp": xp}, {"tp": lax.rem(z + 1, 4)}, {"tp": lax.rem(z + 3, 4)}])
 
-    def item_start(i, own, across):
-        return own * PIECES + i if i < PIECES else across * PIECES + FIRST + i - PIECES
+    def span(owner, i, count=1):
+        return pl.ds(pl.multiple_of(owner * rows + offsets[i], unit), sum(sizes[i:i + count]))
+
+    def item_span(i, own, across):
+        return span(own, i) if i < PIECES else span(across, FIRST + i - PIECES)
 
     def item_rows(i):
-        return aligned(item_start(i, sp, yp), piece)
+        return item_span(i, sp, yp)
 
     def block(i, k):
         return xf.at[item_rows(i), aligned(k, cols)]
@@ -100,7 +108,7 @@
             to_core(i, z + s)
 
     def w_rows(quarter, x_half, c):
-        return aligned((quarter * 2 + x_half) * WCHUNKS + c, chunk)
+        return aligned((quarter * 2 + x_half) * QKV_CHUNKS + c, chunk)
 
     def w_recv(n):
         source = (yp, ycp)[n % 2]
@@ -120,9 +128,9 @@
     for j in range(late):
         i = FIRST + j
         send(block(i, z), block(i, z), ys.at[j], yr.at[j], sp=yp)
-    for n in range(2 * WCHUNKS):
+    for n in range(2 * QKV_CHUNKS):
         target = (yp, ycp)[n % 2]
-        local = aligned(dp * WCHUNKS + n // 2, chunk)
+        local = aligned(dp * QKV_CHUNKS + n // 2, chunk)
         send(w_ref.at[local, aligned(target, group)], wf.at[w_rows(sp, dp, n // 2), :],
              ys.at[late + n], yr.at[late + n], sp=target)
     for i in range(PIECES):
@@ -141,118 +149,117 @@
 
     def q_send(i):
         ref = xf.at[item_rows(i), :]
-        send(ref, ref, ys.at[late + 2 * WCHUNKS + i], yr.at[late + 2 * WCHUNKS + i], sp=yp)
-
-    def q_rows(i, owner):
-        return aligned(owner * PIECES + i, piece)
+        send(ref, ref, ys.at[late + 2 * QKV_CHUNKS + i], yr.at[late + 2 * QKV_CHUNKS + i], sp=yp)
 
     def q_recv(i):
-        ref = xf.at[q_rows(i, yp), :]
-        wait_bytes(ref, yr.at[late + 2 * WCHUNKS + i])
+        ref = xf.at[span(yp, i), :]
+        wait_bytes(ref, yr.at[late + 2 * QKV_CHUNKS + i])
         send(ref, ref, ds.at[items + i], dr.at[items + i], sp=cp)
 
     z_recv(0, 1)
     for j in range(late):
         y_recv(j)
     z_recv(1, 1)
+    w_recv(0)
+    w_recv(1)
     z_recv(2, 1)
-    w_recv(0)
+    w_recv(2)
     z_recv(3, 1)
-    w_recv(1)
-    for i in range(PIECES, items):
-        z_recv(i, 1)
-    w_recv(2)
+    w_recv(3)
+    w_recv(4)
+    z_recv(4, 1)
+    w_recv(5)
+    z_recv(5, 1)
+    w_recv(6)
     z_recv(0, 2)
+    w_recv(7)
     z_recv(1, 2)
-    w_recv(3)
+    w_recv(8)
     z_recv(2, 2)
-    w_recv(4)
+    w_recv(9)
     z_recv(3, 2)
-    w_recv(5)
-    for i in range(PIECES, items):
-        z_recv(i, 2)
-    w_recv(6)
-    for i in range(FIRST):
-        z_recv(i, 3)
-        q_send(i)
-    w_recv(7)
+    w_recv(10)
+    w_recv(11)
+    z_recv(4, 2)
+    w_recv(12)
+    z_recv(5, 2)
+    w_recv(13)
+    z_recv(0, 3)
+    q_send(0)
+    w_recv(14)
+    z_recv(1, 3)
+    q_send(1)
+    w_recv(15)
 
     tile = 512 if group % 512 == 0 else group
-    count = [0]
-
-    def matmul(start, size):
-        slot = count[0] % 2
-        span = aligned(start, size)
-        if count[0] >= 2:
-            wait_bytes(stage.at[slot, pl.ds(0, sizes[count[0] - 2]), :], outs.at[slot])
-        sizes.append(size)
+    done = []
+
+    def matmul(where):
+        slot = len(done) % 2
+        if len(done) >= 2:
+            wait_bytes(stage.at[slot, pl.ds(0, done[-2]), :], outs.at[slot])
+        size = where.size
+        done.append(size)
 
         def step(n, carry):
             at = aligned(n, tile)
             stage[slot, 0:size, at] = jnp.dot(
-                xf[span, :], wf[:, at], preferred_element_type=jnp.float32).astype(jnp.bfloat16)
+                xf[where, :], wf[:, at], preferred_element_type=jnp.float32).astype(jnp.bfloat16)
             return carry
 
         lax.fori_loop(0, group // tile, step, 0)
-        pltpu.make_async_copy(stage.at[slot, pl.ds(0, size), :], qkv_ref.at[span, :], outs.at[slot]).start()
-        count[0] += 1
-
-    sizes = []
-
-    def core_rows(i):
-        if i < items:
-            return aligned(item_start(i, cp, ycp), piece)
-        return q_rows(i - items, ycp)
+        pltpu.make_async_copy(stage.at[slot, pl.ds(0, size), :], qkv_ref.at[where, :], outs.at[slot]).start()
 
     def from_core(i):
-        wait_bytes(xf.at[core_rows(i), :], dr.at[i])
+        where = item_span(i, cp, ycp) if i < items else span(ycp, i - items)
+        wait_bytes(xf.at[where, :], dr.at[i])
 
     w_own.wait()
     wait_bytes(wf.at[aligned(cp, depth), :], dr.at[items + FIRST])
     for n, source in enumerate((yp, ycp)):
         wait_bytes(wf.at[aligned(source * 2 + xp, half), :], xr.at[n])
 
-    unit = FIRST * piece
-    assert FIRST == late
-    matmul(sp * 2, unit)
+    matmul(span(sp, 0, 2))
+    z_recv(2, 3)
     for i in range(FIRST):
         from_core(i)
-    for i in range(FIRST, PIECES):
-        z_recv(i, 3)
-    matmul(cp * 2, unit)
-    for i in range(PIECES, items):
-        z_recv(i, 3)
-    matmul(sp * 2 + 1, unit)
+    matmul(span(cp, 0, 2))
+    z_recv(3, 3)
+    matmul(span(sp, 2, 2))
     q_recv(0)
-    for i in range(FIRST, PIECES):
-        from_core(i)
-    matmul(cp * 2 + 1, unit)
-    for i in range(PIECES, items):
-        from_core(i)
-    matmul(yp * 2 + 1, unit)
-    matmul(ycp * 2 + 1, unit)
-    for i in range(1, FIRST):
-        q_recv(i)
-    matmul(yp * 2, unit)
-    for i in range(FIRST):
-        from_core(items + i)
-    matmul(ycp * 2, unit)
-
-    for slot in range(2):
-        wait_bytes(stage.at[slot, pl.ds(0, unit), :], outs.at[slot])
+    z_recv(4, 3)
+    from_core(2)
+    from_core(3)
+    matmul(span(cp, 2, 2))
+    z_recv(5, 3)
+    from_core(4)
+    matmul(span(yp, 2))
+    matmul(span(ycp, 2))
+    q_recv(1)
+    from_core(5)
+    matmul(span(yp, 3))
+    matmul(span(ycp, 3))
+    matmul(span(yp, 0, 2))
+    from_core(items)
+    from_core(items + 1)
+    matmul(span(ycp, 0, 2))
+
+    for back in (2, 1):
+        slot = (len(done) - back) % 2
+        wait_bytes(stage.at[slot, pl.ds(0, done[-back]), :], outs.at[slot])
     seg_own.wait()
     for n, peer in enumerate((cp, yp, ycp)):
         wait_bytes(seg_ref, gs.at[n])
         wait_bytes(segs_ref.at[peer], gr.at[n])
     for j in range(late):
         wait_bytes(block(FIRST + j, z), ys.at[j])
-    for n in range(2 * WCHUNKS):
+    for n in range(2 * QKV_CHUNKS):
         ref = wf.at[pl.ds(0, chunk), :]
         wait_bytes(ref, ys.at[late + n])
         wait_bytes(ref, xs.at[n])
     for i in range(FIRST):
-        wait_bytes(xf.at[item_rows(i), :], ys.at[late + 2 * WCHUNKS + i])
-        wait_bytes(xf.at[q_rows(i, yp), :], ds.at[items + i])
+        wait_bytes(xf.at[item_rows(i), :], ys.at[late + 2 * QKV_CHUNKS + i])
+        wait_bytes(xf.at[span(yp, i), :], ds.at[items + i])
     for i in range(items):
         wait_bytes(xf.at[item_rows(i), :], ds.at[i])
         for s in range(1, 4):
@@ -272,7 +279,7 @@
     group = width // 4
     late = PIECES - FIRST
     items = PIECES + late
-    crossings = late + 2 * WCHUNKS + FIRST
+    crossings = late + 2 * QKV_CHUNKS + FIRST
     dma = pltpu.SemaphoreType.DMA
     any_space = pl.BlockSpec(memory_space=pl.ANY)
     return pl.pallas_call(
@@ -286,13 +293,13 @@
         scratch_shapes=[
             pltpu.VMEM((4 * rows, 4 * cols), jnp.bfloat16),
             pltpu.VMEM((4 * depth, group), jnp.bfloat16),
-            pltpu.VMEM((2, FIRST * rows // PIECES, group), jnp.bfloat16),
+            pltpu.VMEM((2, rows * sum(SHARES[FIRST:]) // 16, group), jnp.bfloat16),
             dma((3,)),
             dma((crossings,)),
             dma((crossings,)),
             dma((items, 2, 3)),
             dma((items, 2, 3)),
-            dma((2 * WCHUNKS,)),
+            dma((2 * QKV_CHUNKS,)),
             dma((2,)),
             dma((items + FIRST + 1,)),
             dma((items + FIRST + 1,)),
@@ -305,48 +312,35 @@
     )(x, seg, w)
 
 
-def attention_kernel(q_ref, k_ref, v_ref, segq_ref, segk_ref, o_ref):
-    scores = lax.dot_general(q_ref[...], k_ref[...], (((1,), (1,)), ((), ())), preferred_element_type=jnp.float32)
-    scores = jnp.where(segq_ref[...] == segk_ref[...], scores * SOFTMAX_SCALE, -jnp.inf)
+def attend(q, k, v, same):
+    scores = lax.dot_general(q, k, (((1,), (1,)), ((), ())), preferred_element_type=jnp.float32)
+    scores = jnp.where(same, scores, -jnp.inf)
     top = jnp.max(scores, axis=1, keepdims=True)
-    weights = jnp.exp(scores - top)
-    weights = (weights / jnp.sum(weights, axis=1, keepdims=True)).astype(jnp.bfloat16)
-    o_ref[...] = jnp.dot(weights, v_ref[...], preferred_element_type=jnp.float32).astype(jnp.bfloat16)
-
-
-def attention(qkv, segs):
-    tokens, width = qkv.shape
-    heads = width // (3 * HEAD_DIM)
-    block = min(256, tokens)
-    return pl.pallas_call(
-        attention_kernel,
-        out_shape=jax.ShapeDtypeStruct((tokens, heads * HEAD_DIM), jnp.bfloat16),
-        grid=(heads, tokens // block),
-        in_specs=[
-            pl.BlockSpec((block, HEAD_DIM), lambda h, i: (i, 3 * h)),
-            pl.BlockSpec((tokens, HEAD_DIM), lambda h, i: (0, 3 * h + 1)),
-            pl.BlockSpec((tokens, HEAD_DIM), lambda h, i: (0, 3 * h + 2)),
-            pl.BlockSpec((block, 1), lambda h, i: (i, 0)),
-            pl.BlockSpec((1, tokens), lambda h, i: (0, 0)),
-        ],
-        out_specs=pl.BlockSpec((block, HEAD_DIM), lambda h, i: (i, h)),
-        name="attention",
-    )(qkv, qkv, qkv, segs.reshape(tokens, 1), segs.reshape(1, tokens))
-
-
-def out_kernel(o_ref, w_ref, y_ref, of, wf, acc, stage,
+    weights = jnp.exp2((scores - top) * (SOFTMAX_SCALE * LOG2_E))
+    inverse = 1.0 / jnp.sum(weights, axis=1, keepdims=True)
+    weights = (weights * inverse).astype(jnp.bfloat16)
+    return jnp.dot(weights, v, preferred_element_type=jnp.float32).astype(jnp.bfloat16)
+
+
+def out_kernel(qkv_ref, segq_ref, segk_ref, w_ref, y_ref, qv, ov, of, wf, acc, stage,
                loc, os, orr, zs, zr, ys, yr, xs, xr, ds, dr, fs, fr, outl):
     dp, z, sp = lax.axis_index("dp"), lax.axis_index("tp"), lax.axis_index("sp")
     cp, yp, ycp = sp_peers(sp)
     xp = 1 - dp
     y = sp // 2
-    tokens, width = o_ref.shape
+    tokens = qkv_ref.shape[0]
+    width = qkv_ref.shape[1] // 3
+    heads = width // HEAD_DIM
     rows = tokens // 4
     depth, cols = w_ref.shape
     half = depth // 2
-    chunk = half // WCHUNKS
+    chunk = half // OUT_CHUNKS
     sources = (sp, cp, yp, ycp)
 
+    qkv_in = pltpu.make_async_copy(qkv_ref, qv, loc.at[0])
+    qkv_in.start()
+    w_own = pltpu.make_async_copy(w_ref, wf.at[aligned(sp, depth), :], loc.at[1])
+    w_own.start()
     enter([{"sp": cp}, {"sp": yp}, {"sp": ycp}, {"dp": xp}] + [{"tp": lax.rem(z + r, 4)} for r in (1, 2, 3)])
 
     def block(j, k):
@@ -378,7 +372,7 @@
                 z_send(j, 1, s + 1)
 
     def w_rows(quarter, x_half, c):
-        return aligned((quarter * 2 + x_half) * WCHUNKS + c, chunk)
+        return aligned((quarter * 2 + x_half) * OUT_CHUNKS + c, chunk)
 
     def w_recv(n):
         ref = wf.at[w_rows(yp, dp, n), :]
@@ -391,37 +385,69 @@
         wait_bytes(ref, xr.at[n])
         send(ref, ref, ds.at[2], dr.at[2], sp=cp)
 
-    o_own = pltpu.make_async_copy(o_ref.at[aligned(sp, rows), :], block(0, z), loc.at[0])
-    o_own.start()
-    for n, peer in enumerate((cp, yp, ycp)):
-        send(o_ref.at[aligned(peer, rows), :], block(0, z), os.at[n], orr.at[n], sp=peer)
-    for n in range(WCHUNKS):
-        send(w_ref.at[aligned(dp * WCHUNKS + n, chunk), :], wf.at[w_rows(sp, dp, n), :], ys.at[n], yr.at[n], sp=yp)
-    o_own.wait()
-    z_send(0, 0, 1)
-    z_send(0, 1, 1)
-    w_own = pltpu.make_async_copy(w_ref, wf.at[aligned(sp, depth), :], loc.at[1])
-    w_own.start()
-    for n in range(3):
+    def w_send(n):
+        send(w_ref.at[aligned(dp * OUT_CHUNKS + n, chunk), :], wf.at[w_rows(sp, dp, n), :], ys.at[n], yr.at[n], sp=yp)
+
+    queries = min(256, rows)
+    spans = rows // queries
+
+    def attention(owner, store):
+        def step(t, carry):
+            h, b = t // spans, lax.rem(t, spans)
+            at = aligned(owner * spans + b, queries)
+            same = segq_ref[at, :] == segk_ref[...]
+            store(h, aligned(b, queries), attend(
+                qv[at, aligned(3 * h, HEAD_DIM)], qv[:, aligned(3 * h + 1, HEAD_DIM)],
+                qv[:, aligned(3 * h + 2, HEAD_DIM)], same))
+            return carry
+
+        lax.fori_loop(0, heads * spans, step, 0)
+
+    def store_own(h, at, value):
+        of[at, aligned((z * 4 + sp) * heads + h, HEAD_DIM)] = value
+
+    def attend_for(n):
+        def store(h, at, value):
+            ov[n, at, aligned(h, HEAD_DIM)] = value
+
+        peer = sources[n + 1]
+        attention(peer, store)
+        send(ov.at[n], block(0, z), os.at[n], orr.at[n], sp=peer)
+
+    def o_recv(n):
         wait_bytes(block(1 + n, z), orr.at[n])
         z_send(1 + n, 0, 1)
         z_send(1 + n, 1, 1)
-        if n == 0:
-            send(w_ref, wf.at[aligned(sp, depth), :], ds.at[0], dr.at[0], sp=cp)
-            acc[...] = jnp.zeros_like(acc)
-            z_recv(0, 1)
+
+    w_send(0)
+    send(w_ref, wf.at[aligned(sp, depth), :], ds.at[0], dr.at[0], sp=cp)
+    qkv_in.wait()
+    attention(sp, store_own)
+    z_send(0, 0, 1)
+    z_send(0, 1, 1)
+    attend_for(1)
+    z_recv(0, 1)
+    attend_for(2)
+    for n in range(1, OUT_CHUNKS):
+        w_send(n)
+    o_recv(1)
+    attend_for(0)
+    o_recv(2)
+    o_recv(0)
+    w_recv(0)
+    z_recv(0, 2)
+    acc[...] = jnp.zeros_like(acc)
+    z_recv(2, 1)
+    z_recv(0, 3)
+    z_recv(3, 1)
+    w_recv(1)
     z_recv(1, 1)
-    z_recv(2, 1)
-    w_recv(0)
-    z_recv(3, 1)
-    z_recv(0, 2)
-    w_recv(1)
-    z_recv(1, 2)
     x_recv(0)
     z_recv(2, 2)
+    z_recv(3, 2)
     w_recv(2)
-    z_recv(3, 2)
     x_recv(1)
+    z_recv(1, 2)
 
     tile = min(512, cols)
     tiles = cols // tile
@@ -445,14 +471,13 @@
 
     w_own.wait()
     wait_bytes(wf.at[aligned(cp, depth), :], dr.at[0])
-    z_recv(0, 3)
     near_blocks(lambda gap: (gap <= 2) & (gap >= -2))
+    z_recv(2, 3)
     w_recv(3)
+    x_recv(2)
+    z_recv(3, 3)
+    x_recv(3)
     z_recv(1, 3)
-    x_recv(2)
-    z_recv(2, 3)
-    x_recv(3)
-    z_recv(3, 3)
     near_blocks(lambda gap: (gap > 2) | (gap < -2))
     for n in range(2):
         wait_bytes(wf.at[aligned(ycp * 2 + (dp, xp)[n], half), :], dr.at[1 + n])
@@ -475,8 +500,8 @@
         wait_bytes(stage.at[aligned(z, part), :], fs.at[r - 1])
     wait_bytes(y_ref.at[:, aligned(z, cols)], outl.at[0])
     for n, peer in enumerate((cp, yp, ycp)):
-        wait_bytes(block(0, z), os.at[n])
-    for n in range(WCHUNKS):
+        wait_bytes(ov.at[n], os.at[n])
+    for n in range(OUT_CHUNKS):
         ref = wf.at[pl.ds(0, chunk), :]
         wait_bytes(ref, ys.at[n])
         wait_bytes(ref, xs.at[n])
@@ -494,8 +519,8 @@
                 wait_bytes(block(j, z), zs.at[j, 1, s - 1])
 
 
-def project_out(o, w):
-    tokens, width = o.shape
+def attend_project(qkv, segs, w):
+    tokens, width = qkv.shape[0], qkv.shape[1] // 3
     rows = tokens // 4
     depth, cols = w.shape
     dma = pltpu.SemaphoreType.DMA
@@ -503,9 +528,11 @@
     return pl.pallas_call(
         out_kernel,
         out_shape=jax.ShapeDtypeStruct((rows // 4, 4 * cols), jnp.bfloat16),
-        in_specs=[any_space] * 2,
+        in_specs=[any_space] + [pl.BlockSpec(memory_space=pltpu.VMEM)] * 2 + [any_space],
         out_specs=any_space,
         scratch_shapes=[
+            pltpu.VMEM(qkv.shape, jnp.bfloat16),
+            pltpu.VMEM((3, rows, width), jnp.bfloat16),
             pltpu.VMEM((rows, 4 * depth), jnp.bfloat16),
             pltpu.VMEM((4 * depth, cols), jnp.bfloat16),
             pltpu.VMEM((rows, cols), jnp.float32),
@@ -515,10 +542,10 @@
             dma((3,)),
             dma((4, 2, 3)),
             dma((4, 2, 3)),
-            dma((WCHUNKS,)),
-            dma((WCHUNKS,)),
-            dma((WCHUNKS,)),
-            dma((WCHUNKS,)),
+            dma((OUT_CHUNKS,)),
+            dma((OUT_CHUNKS,)),
+            dma((OUT_CHUNKS,)),
+            dma((OUT_CHUNKS,)),
             dma((3,)),
             dma((3,)),
             dma((3,)),
@@ -526,8 +553,8 @@
             dma((1,)),
         ],
         compiler_params=pltpu.CompilerParams(collective_id=1, has_side_effects=True, vmem_limit_bytes=VMEM_LIMIT),
-        name="project_out",
-    )(o, w)
+        name="attend_project",
+    )(qkv, segs.reshape(tokens, 1), segs.reshape(1, tokens), w)
 
 
 def solution(mesh):
@@ -536,7 +563,7 @@
 
     def device_block(x_block, doc_block, wqkv_block, wout_block):
         qkv, segs = gather_qkv(x_block, doc_block.reshape(-1, HEAD_DIM), wqkv_block)
-        return project_out(attention(qkv, segs), wout_block)
+        return attend_project(qkv, segs, wout_block)
 
     return jax.shard_map(
         device_block,

time: 511 us -> 462 us (0.904)
  Pallas kernels: 503 us -> 456 us
    pallas_call x2 -> x1, Pallas kernels: 230 us -> 195 us  [attend_project(): pl.pallas_call(out_kernel, out_shape=jax.ShapeDtypeStruct((rows // 4, 4 *...]
    pallas_call x1, Pallas kernels: 272 us -> 261 us  [gather_qkv(): pl.pallas_call(qkv_kernel, out_shape=(jax.ShapeDtypeStruct((4 * rows, gro...]
where the time goes in v2:
time: 462 us
  Pallas kernels  456 us (99%)
  local copies, waits for them, and re-layouts  5.13 us (1%)
    pallas_call x1, Pallas kernels, gather_qkv(): pl.pallas_call(qkv_kernel, out_shape=(jax.ShapeDtypeStruct((4 * rows, gro...  261 us
    pallas_call x1, Pallas kernels, attend_project(): pl.pallas_call(out_kernel, out_shape=jax.ShapeDtypeStruct((rows // 4, 4 *...  195 us

profile of v2, /device:TPU:0, one launch (start us, length us, event | category | flops | bytes accessed | tf_op | source)
XLA Modules:
  0.0 461.6 jit_solution(9231587162967894070)
XLA Ops:
  0.0 261.4 %gather_qkv.1 = (bf16[2048,1536]{1,0:T(8,128)(2,1)}, s32[4,4,128]{2,1,0:T(4,128)}) custom-call(bf16[512,2048]{1,0:T(8,128)(2,1)} %x_ref.1, s32[4,128]{1,0:T(4,128)} %bitcast.5, bf16[2048,6144]{1,0:T(8,128)(2,1)} %w_ref.2), custom_call_target="tpu_custom_call" | custom-call | tf_op jit(solution)/shard_map/gather_qkv/pallas_call | solution.py:285
  261.4 2.0 copy.5.segq_ref
  263.4 195.0 %attend_project.1 = bf16[128,8192]{1,0:T(8,128)(2,1)} custom-call(bf16[2048,1536]{1,0:T(8,128)(2,1)} %get-tuple-element.7.qkv_ref, s32[2048,1]{1,0:T(8,128)} %copy.5.segq_ref, s32[1,2048]{1,0:T(1,128)} %bitcast.4, bf16[2048,2048]{1,0:T(8,128)(2,1)} %w_ref.3), custom_call_target="tpu_custom_call" | custom-call | tf_op jit(solution)/shard_map/attend_project/pallas_call | solution.py:528
  458.5 3.1 copy.7

commit v3 on v0

v3 whole, which is shorter than its diff:
```python
import jax
import jax.numpy as jnp
from jax import lax
from jax.experimental import pallas as pl
from jax.experimental.pallas import tpu as pltpu
from jax.sharding import PartitionSpec as P

HEAD_DIM = 128
HEAD_COLS = 3 * HEAD_DIM
SOFTMAX_SCALE = HEAD_DIM ** -0.5
LOG2_E = 1.4426950408889634
MESH = pl.DeviceIdType.MESH
VMEM_LIMIT = 67_000_000

PIECES = 4
FIRST = 2
SHARES = (5, 4, 4, 3)
HEADS = 4
GROUPS = ((0, 2), (2, 1), (3, 1))
CHUNKS = (4, 2, 2)
W_BASE = (0, 8, 12)
TILES = 4
QKV_STEPS = 8


def send(src, dst, ssem, rsem, **device):
    copy = pltpu.make_async_remote_copy(
        src_ref=src, dst_ref=dst, send_sem=ssem, recv_sem=rsem, device_id=device, device_id_type=MESH
    )
    copy.start()


def local(src, dst, sem):
    copy = pltpu.make_async_copy(src, dst, sem)
    copy.start()
    return copy


def wait_bytes(ref, sem):
    pltpu.make_async_copy(ref, ref, sem).wait()


def enter(peers):
    barrier = pltpu.get_barrier_semaphore()
    for peer in peers:
        pl.semaphore_signal(barrier, inc=1, device_id=peer, device_id_type=MESH)
    pl.semaphore_wait(barrier, len(peers))


def aligned(index, size):
    return pl.ds(pl.multiple_of(index * size, size), size)


def columns(start, size):
    return pl.ds(pl.multiple_of(start, HEAD_DIM), size)


def attend(q, k, v, same):
    scores = lax.dot_general(q, k, (((1,), (1,)), ((), ())), preferred_element_type=jnp.float32)
    scores = jnp.where(same, scores, -jnp.inf)
    top = jnp.max(scores, axis=1, keepdims=True)
    weights = jnp.exp2((scores - top) * (SOFTMAX_SCALE * LOG2_E))
    inverse = 1.0 / jnp.sum(weights, axis=1, keepdims=True)
    weights = (weights * inverse).astype(jnp.bfloat16)
    return jnp.dot(weights, v, preferred_element_type=jnp.float32).astype(jnp.bfloat16)


def block_kernel(x_ref, seg_ref, w_ref, wo_ref, y_ref, xall, woall,
                 xs, wf, qv, of, ov, stage, segs, segcol, segrow,
                 loc, seg_s, seg_r, xy_s, xy_r, xz_s, xz_r, xd_s, xd_r,
                 wy_s, wy_r, wx_s, wx_r, wd_s, wd_r,
                 op_s, op_r, oz_s, oz_r,
                 vy_s, vy_r, vx_s, vx_r, vd_s, vd_r, vl, f_s, f_r):
    dp, z, sp = lax.axis_index("dp"), lax.axis_index("tp"), lax.axis_index("sp")
    core, y = lax.rem(sp, 2), sp // 2
    cp, yp, ycp = sp + 1 - 2 * core, lax.rem(sp + 2, 4), 3 - sp
    xp = 1 - dp
    sources = (sp, cp, yp, ycp)
    rows, cols = x_ref.shape
    tokens = 4 * rows
    depth = w_ref.shape[0]
    half = depth // 2
    width = HEADS * HEAD_DIM
    unit = rows // 16
    sizes = [share * unit for share in SHARES]
    offsets = [sum(sizes[:i]) for i in range(PIECES)]
    late = PIECES - FIRST
    items = PIECES + late

    def span(owner, i, count=1):
        return pl.ds(pl.multiple_of(owner * rows + offsets[i], unit), sum(sizes[i:i + count]))

    def item_span(i, own, across):
        return span(own, i) if i < PIECES else span(across, FIRST + i - PIECES)

    def x_block(i, k):
        return xall.at[item_span(i, sp, yp), aligned(k, cols)]

    def x_source(i, k, own):
        return x_ref.at[pl.ds(offsets[i], sizes[i]), :] if own and i < PIECES else x_block(i, k)

    def x_core(i, k, own=False):
        send(x_source(i, k, own), x_block(i, k), xd_s.at[i], xd_r.at[i], sp=cp)

    def line_send(copy, s_sem, r_sem, d, s):
        if d == 0:
            @pl.when((z <= 2) & (z >= s - 1))
            def _():
                k = z - (s - 1)
                send(copy[0](k), copy[1](k), s_sem.at[d, s - 1], r_sem.at[d, s - 1], tp=z + 1)
        else:
            @pl.when((z >= 1) & (z + s - 1 <= 3))
            def _():
                k = z + (s - 1)
                send(copy[0](k), copy[1](k), s_sem.at[d, s - 1], r_sem.at[d, s - 1], tp=z - 1)

    def x_line(i, d, s):
        line_send((lambda k: x_source(i, k, s == 1), lambda k: x_block(i, k)), xz_s.at[i], xz_r.at[i], d, s)

    def x_first(i):
        x_line(i, 0, 1)
        x_line(i, 1, 1)

    def x_recv(i, s):
        @pl.when(z >= s)
        def _():
            wait_bytes(x_block(i, z - s), xz_r.at[i, 0, s - 1])
            if s < 3:
                x_line(i, 0, s + 1)
            x_core(i, z - s)

        @pl.when(z + s <= 3)
        def _():
            wait_bytes(x_block(i, z + s), xz_r.at[i, 1, s - 1])
            if s < 3:
                x_line(i, 1, s + 1)
            x_core(i, z + s)

    def p_recv(j):
        wait_bytes(x_block(PIECES + j, z), xy_r.at[j])
        x_core(PIECES + j, z)

    def q_send(i):
        ref = xall.at[span(sp, i), :]
        send(ref, ref, xy_s.at[late + i], xy_r.at[late + i], sp=yp)

    def q_recv(i):
        ref = xall.at[span(yp, i), :]
        wait_bytes(ref, xy_r.at[late + i])
        send(ref, ref, xd_s.at[items + i], xd_r.at[items + i], sp=cp)

    def from_core(i):
        where = item_span(i, cp, ycp) if i < items else span(ycp, i - items)
        wait_bytes(xall.at[where, :], xd_r.at[i])

    def group_cols(g, owner=0):
        first, count = GROUPS[g]
        return columns((owner * HEADS + first) * HEAD_COLS, count * HEAD_COLS)

    def w_rows(quarter, x_half, g, c):
        return aligned((quarter * 2 + x_half) * CHUNKS[g] + c, half // CHUNKS[g])

    def w_send(g):
        for c in range(2 * CHUNKS[g]):
            target = (yp, ycp)[c % 2]
            send(w_ref.at[aligned(dp * CHUNKS[g] + c // 2, half // CHUNKS[g]), group_cols(g, target)],
                 wf.at[w_rows(sp, dp, g, c // 2), group_cols(g)],
                 wy_s.at[W_BASE[g] + c], wy_r.at[W_BASE[g] + c], sp=target)

    def w_recv(g, c):
        ref = wf.at[w_rows((yp, ycp)[c % 2], dp, g, c // 2), group_cols(g)]
        wait_bytes(ref, wy_r.at[W_BASE[g] + c])
        send(ref, ref, wx_s.at[W_BASE[g] + c], wx_r.at[2 * g + c % 2], dp=xp)

    def w_ready(g):
        for n, source in enumerate((yp, ycp)):
            wait_bytes(wf.at[aligned(source * 2 + xp, half), group_cols(g)], wx_r.at[2 * g + n])

    split = (columns(0, 2 * HEAD_COLS), columns(2 * HEAD_COLS, 2 * HEAD_COLS))

    def w_core(n):
        send(w_ref.at[:, columns((cp * HEADS + 2 * n) * HEAD_COLS, 2 * HEAD_COLS)],
             wf.at[aligned(sp, depth), split[n]], wd_s.at[n], wd_r.at[n], sp=cp)

    def w_from_core(n):
        wait_bytes(wf.at[aligned(cp, depth), split[n]], wd_r.at[n])

    def load(where, slot):
        local(xall.at[where, :], xs.at[slot, pl.ds(0, where.size), :], loc.at[4 + slot])

    def go(where, slot):
        size = where.size
        wait_bytes(xs.at[slot, pl.ds(0, size), :], loc.at[4 + slot])

        def step(n, carry):
            at = aligned(n, 2 * HEAD_DIM)
            qv[where, at] = jnp.dot(xs[slot, 0:size, :], wf[0:4 * depth, at],
                                    preferred_element_type=jnp.float32).astype(jnp.bfloat16)
            return carry

        lax.fori_loop(0, GROUPS[0][1] * HEAD_COLS // (2 * HEAD_DIM), step, 0)

    def qkv(where, slot):
        load(where, slot)
        go(where, slot)

    def at_step(n, events):
        for k, acts in events.items():
            @pl.when(n == k)
            def _():
                for act, *args in acts:
                    act(*args)

    part = tokens // QKV_STEPS

    def qkv_group(g, events):
        first, count = GROUPS[g]
        at = pl.ds(first * HEAD_COLS, count * HEAD_COLS)
        load(aligned(0, part), 0)

        def step(n, carry):
            slot = lax.rem(n, 2)

            @pl.when(n + 1 < QKV_STEPS)
            def _():
                local(xall.at[aligned(n + 1, part), :], xs.at[1 - slot, pl.ds(0, part), :], loc.at[5 - slot])

            wait_bytes(xs.at[slot, pl.ds(0, part), :], loc.at[4 + slot])
            qv[aligned(n, part), at] = jnp.dot(xs[slot, 0:part, :], wf[0:4 * depth, at],
                                               preferred_element_type=jnp.float32).astype(jnp.bfloat16)
            at_step(n, events)
            return carry

        lax.fori_loop(0, QKV_STEPS, step, 0)

    def o_block(g, j, k):
        first, count = GROUPS[g]
        return of.at[:, columns(((k * 4 + sources[j]) * HEADS + first) * HEAD_DIM, count * HEAD_DIM)]

    def o_line(g, j, d, s):
        item = 4 * g + j
        line_send((lambda k: o_block(g, j, k),) * 2, oz_s.at[item], oz_r.at[item], d, s)

    def o_first(g, j):
        o_line(g, j, 0, 1)
        o_line(g, j, 1, 1)

    def o_recv(g, j):
        wait_bytes(o_block(g, j, z), op_r.at[3 * g + j - 1])
        o_first(g, j)

    def o_next(g, j, s):
        @pl.when(z >= s)
        def _():
            wait_bytes(o_block(g, j, z - s), oz_r.at[4 * g + j, 0, s - 1])
            if s < 3:
                o_line(g, j, 0, s + 1)

        @pl.when(z + s <= 3)
        def _():
            wait_bytes(o_block(g, j, z + s), oz_r.at[4 * g + j, 1, s - 1])
            if s < 3:
                o_line(g, j, 1, s + 1)

    queries = min(256, rows)
    spans = rows // queries
    order = (0, 2, 3, 1)

    def attention(g, events):
        first, count = GROUPS[g]
        here = pl.ds(first * HEAD_DIM, count * HEAD_DIM)

        def quarter(n, carry):
            owner = 2 * lax.rem(y + lax.rem((n + 1) // 2, 2), 2) + lax.rem(core + n // 2, 2)

            def step(t, carry):
                h, b = first + t // spans, lax.rem(t, spans)
                at = aligned(owner * spans + b, queries)
                ov[n, aligned(b, queries), aligned(h, HEAD_DIM)] = attend(
                    qv[at, aligned(3 * h, HEAD_DIM)], qv[:, aligned(3 * h + 1, HEAD_DIM)],
                    qv[:, aligned(3 * h + 2, HEAD_DIM)], segcol[at, 0:1] == segrow[...])
                return carry

            lax.fori_loop(0, count * spans, step, 0)

            @pl.when(n == 0)
            def _():
                of[:, columns(((z * 4 + sp) * HEADS + first) * HEAD_DIM, count * HEAD_DIM)] = ov[0, :, here]
                o_first(g, 0)

            for k in range(1, 4):
                @pl.when(n == k)
                def _():
                    j = order[k]
                    send(ov.at[k, :, here], o_block(g, 0, z), op_s.at[3 * g + j - 1], op_r.at[3 * g + j - 1],
                         sp=sources[j])

            at_step(n, events)
            return carry

        lax.fori_loop(0, 4, quarter, 0)

    o_depth, out_cols = wo_ref.shape
    o_half = o_depth // 2
    tile = out_cols // TILES

    def v_block(quarter, x_half, c):
        return (aligned((quarter * 2 + x_half) * 2 + c % 2, o_half // 2), pl.ds(c // 2 * tile, tile))

    def v_send(c):
        at = v_block(sp, dp, c)
        send(wo_ref.at[aligned(dp * 2 + c % 2, o_half // 2), pl.ds(c // 2 * tile, tile)], woall.at[at],
             vy_s.at[c], vy_r.at[c], sp=yp)

    def v_recv(c):
        ref = woall.at[v_block(yp, dp, c)]
        wait_bytes(ref, vy_r.at[c])
        send(ref, ref, vx_s.at[c], vx_r.at[c], dp=xp)
        send(ref, ref, vd_s.at[c // 2], vd_r.at[c // 2], sp=cp)

    def v_from_x(c):
        ref = woall.at[v_block(yp, xp, c)]
        wait_bytes(ref, vx_r.at[c])
        send(ref, ref, vd_s.at[c // 2], vd_r.at[c // 2], sp=cp)

    def v_place(t):
        return pl.ds(t % 3 * tile, tile)

    def v_load(t):
        at = pl.ds(t * tile, tile)
        wait_bytes(woall.at[aligned(ycp, o_depth), at], vd_r.at[t])
        local(wo_ref.at[:, at], wf.at[aligned(sp, o_depth), v_place(t)], vl.at[t])
        for source in (cp, yp, ycp):
            local(woall.at[aligned(source, o_depth), at], wf.at[aligned(source, o_depth), v_place(t)], vl.at[t])

    piece = rows // 4
    narrow = min(tile, 2 * HEAD_DIM)

    def project(t):
        wait_bytes(wf.at[pl.ds(0, 4 * o_depth), v_place(t)], vl.at[t])

        def step(n, carry):
            stage[:, columns(t * tile + n * narrow, narrow)] = jnp.dot(
                of[...], wf[0:4 * o_depth, columns(t % 3 * tile + n * narrow, narrow)],
                preferred_element_type=jnp.float32).astype(jnp.bfloat16)
            return carry

        lax.fori_loop(0, tile // narrow, step, 0)
        at = pl.ds(t * tile, tile)
        there = columns(z * out_cols + t * tile, tile)
        for r in (2, 1, 3):
            to = lax.rem(z + r, 4)
            send(stage.at[aligned(to, piece), at], y_ref.at[:, there], f_s.at[r - 1], f_r.at[r - 1], tp=to)
        local(stage.at[aligned(z, piece), at], y_ref.at[:, there], loc.at[6])

    x_in = local(x_ref, stage.at[:, pl.ds(0, cols)], loc.at[0])
    w_own = local(w_ref.at[:, columns(sp * HEADS * HEAD_COLS, HEADS * HEAD_COLS)], wf.at[aligned(sp, depth), :],
                  loc.at[2])
    seg_own = local(seg_ref, segs.at[sp], loc.at[3])
    enter([{"sp": cp}, {"sp": yp}, {"sp": ycp}, {"dp": xp}] + [{"tp": lax.rem(z + r, 4)} for r in (1, 2, 3)])
    for j in range(late):
        i = FIRST + j
        send(x_source(i, z, True), x_block(i, z), xy_s.at[j], xy_r.at[j], sp=yp)
    for i in range(FIRST):
        x_first(i)
    w_send(0)
    for n, peer in enumerate((cp, yp, ycp)):
        send(seg_ref, segs.at[sp], seg_s.at[n], seg_r.at[n], sp=peer)
    for i in range(PIECES):
        x_core(i, z, True)
    w_core(0)
    x_in.wait()
    x_put = local(stage.at[:, pl.ds(0, cols)], xall.at[aligned(sp, rows), aligned(z, cols)], loc.at[1])

    seg_own.wait()
    for n, peer in enumerate((cp, yp, ycp)):
        wait_bytes(segs.at[peer], seg_r.at[n])
    seg_rows = rows // HEAD_DIM
    for q in range(4):
        for r in range(seg_rows):
            line = segs[q, r:r + 1, :]
            at = (q * seg_rows + r) * HEAD_DIM
            segrow[:, at:at + HEAD_DIM] = line
            segcol[at:at + HEAD_DIM, :] = jnp.broadcast_to(line, (HEAD_DIM, HEAD_DIM)).T
    x_put.wait()

    x_recv(0, 1)
    p_recv(0)
    p_recv(1)
    x_recv(1, 1)
    w_recv(0, 0)
    w_recv(0, 1)
    x_recv(0, 2)
    w_recv(0, 2)
    x_recv(1, 2)
    for i in range(FIRST, items):
        x_first(i)
    w_recv(0, 3)
    w_recv(0, 4)
    x_recv(0, 3)
    q_send(0)
    w_recv(0, 5)
    x_recv(1, 3)
    q_send(1)
    w_send(1)
    w_recv(0, 6)
    w_recv(0, 7)
    w_core(1)
    w_own.wait()
    w_from_core(0)
    w_ready(0)
    qkv(span(sp, 0, 2), 0)
    x_recv(2, 1)
    x_recv(3, 1)
    from_core(0)
    from_core(1)
    qkv(span(cp, 0, 2), 1)
    x_recv(4, 1)
    x_recv(5, 1)
    x_recv(2, 2)
    x_recv(3, 2)
    q_recv(0)
    x_recv(4, 2)
    x_recv(5, 2)
    qkv(span(yp, 0), 0)
    from_core(items)
    qkv(span(ycp, 0), 1)
    x_recv(2, 3)
    x_recv(3, 3)
    from_core(2)
    from_core(3)
    qkv(span(sp, 2, 2), 0)
    qkv(span(cp, 2, 2), 1)
    x_recv(4, 3)
    q_recv(1)
    load(span(yp, 1), 0)
    x_recv(5, 3)
    load(span(yp, 2, 2), 1)
    go(span(yp, 1), 0)
    from_core(items + 1)
    load(span(ycp, 1), 0)
    go(span(yp, 2, 2), 1)
    from_core(4)
    from_core(5)
    load(span(ycp, 2, 2), 1)
    go(span(ycp, 1), 0)
    go(span(ycp, 2, 2), 1)

    attention(0, {
        0: [(w_recv, 1, 0), (w_recv, 1, 1)],
        1: [(o_next, 0, 0, 1), (w_recv, 1, 2)],
        2: [(w_send, 2), (o_next, 0, 0, 2), (w_recv, 1, 3)],
    })
    o_recv(0, 2)
    o_recv(0, 1)
    o_next(0, 0, 3)
    o_recv(0, 3)
    w_from_core(1)
    w_ready(1)
    qkv_group(1, {
        0: [(o_next, 0, 2, 1)],
        1: [(o_next, 0, 1, 1)],
        3: [(o_next, 0, 3, 1)],
        4: [(w_recv, 2, 0)],
        5: [(o_next, 0, 2, 2)],
        6: [(w_recv, 2, 1)],
        7: [(o_next, 0, 1, 2)],
    })
    attention(1, {
        0: [(w_recv, 2, 2)],
        2: [(v_send, 0), (v_send, 1), (v_send, 2)],
        3: [(o_next, 0, 3, 2), (w_recv, 2, 3)],
    })
    send(wo_ref, woall.at[aligned(sp, o_depth), :], vd_s.at[TILES], vd_r.at[TILES], sp=cp)
    o_next(0, 2, 3)
    o_recv(1, 1)
    o_recv(1, 2)
    o_next(0, 1, 3)
    o_recv(1, 3)
    w_ready(2)
    qkv_group(2, {
        0: [(o_next, 0, 3, 3)],
        1: [(o_next, 1, 0, 1)],
        2: [(o_next, 1, 1, 1)],
        3: [(o_next, 1, 2, 1)],
        4: [(o_next, 1, 3, 1), (v_recv, 0)],
        5: [(o_next, 1, 0, 2)],
        6: [(o_next, 1, 1, 2)],
        7: [(o_next, 1, 2, 2)],
    })
    attention(2, {
        0: [(v_recv, 1)],
        1: [(o_next, 1, 3, 2)],
        2: [(v_send, 3), (v_send, 4), (v_send, 5), (v_send, 6), (v_send, 7)],
        3: [(o_next, 1, 0, 3), (v_recv, 2)],
    })
    o_recv(2, 1)
    o_next(1, 1, 3)
    o_next(1, 2, 3)
    o_recv(2, 2)
    o_recv(2, 3)
    o_next(1, 3, 3)

    for c in range(W_BASE[2] + 2 * CHUNKS[2]):
        g = max(g for g in range(3) if W_BASE[g] <= c)
        wait_bytes(wf.at[pl.ds(0, half // CHUNKS[g]), group_cols(g)], wx_s.at[c])
    wait_bytes(woall.at[aligned(cp, o_depth), :], vd_r.at[TILES])
    for j in range(4):
        o_next(2, j, 1)
    v_from_x(0)
    v_from_x(1)
    v_load(0)
    v_recv(3)
    for j in range(4):
        o_next(2, j, 2)
    v_recv(4)
    v_from_x(2)
    v_from_x(3)
    v_load(1)
    for j in range(4):
        o_next(2, j, 3)
    v_recv(5)
    project(0)
    v_from_x(4)
    v_from_x(5)
    v_load(2)
    v_recv(6)
    project(1)
    v_recv(7)
    project(2)
    v_from_x(6)
    v_from_x(7)
    v_load(3)
    project(3)

    for r in (1, 2, 3):
        wait_bytes(y_ref.at[:, aligned(lax.rem(z + 4 - r, 4), out_cols)], f_r.at[r - 1])
        wait_bytes(stage.at[aligned(z, piece), :], f_s.at[r - 1])
    wait_bytes(y_ref.at[:, aligned(z, out_cols)], loc.at[6])
    for n in range(3):
        wait_bytes(seg_ref, seg_s.at[n])
    for j in range(late):
        wait_bytes(x_block(FIRST + j, z), xy_s.at[j])
    for i in range(FIRST):
        wait_bytes(xall.at[span(sp, i), :], xy_s.at[late + i])
        wait_bytes(xall.at[span(yp, i), :], xd_s.at[items + i])
    for c in range(W_BASE[2] + 2 * CHUNKS[2]):
        g = max(g for g in range(3) if W_BASE[g] <= c)
        wait_bytes(wf.at[pl.ds(0, half // CHUNKS[g]), group_cols(g)], wy_s.at[c])
    for n in range(2):
        wait_bytes(wf.at[aligned(sp, depth), split[n]], wd_s.at[n])
    for c in range(2 * TILES):
        ref = woall.at[v_block(yp, dp, c)]
        wait_bytes(ref, vy_s.at[c])
        wait_bytes(ref, vx_s.at[c])
    for t in range(TILES):
        wait_bytes(woall.at[aligned(yp, o_depth), pl.ds(t * tile, tile)], vd_s.at[t])
    wait_bytes(wo_ref, vd_s.at[TILES])
    for g in range(3):
        first, count = GROUPS[g]
        for k in range(1, 4):
            wait_bytes(ov.at[k, :, pl.ds(first * HEAD_DIM, count * HEAD_DIM)], op_s.at[3 * g + order[k] - 1])

    def sent(ref, sems):
        for s in range(1, 4):
            @pl.when((z <= 2) & (z >= s - 1))
            def _():
                wait_bytes(ref, sems.at[0, s - 1])

            @pl.when((z >= 1) & (z + s - 1 <= 3))
            def _():
                wait_bytes(ref, sems.at[1, s - 1])

    for i in range(items):
        wait_bytes(xall.at[item_span(i, sp, yp), :], xd_s.at[i])
        sent(x_block(i, z), xz_s.at[i])
    for g in range(3):
        for j in range(4):
            sent(o_block(g, j, z), oz_s.at[4 * g + j])


def attention_block(x, seg, w, wo):
    rows, cols = x.shape
    depth, group = w.shape[0], w.shape[1] // 4
    o_depth, out_cols = wo.shape
    tokens = 4 * rows
    unit = rows // 16
    items = 2 * PIECES - FIRST
    width = HEADS * HEAD_DIM
    chunks = W_BASE[2] + 2 * CHUNKS[2]
    any_space = pl.BlockSpec(memory_space=pl.ANY)
    longest = max(SHARES[0] + SHARES[1], sum(SHARES[FIRST:])) * unit
    longest = max(longest, tokens // QKV_STEPS)

    def dma(*shape):
        return pltpu.SemaphoreType.DMA(shape)

    y, _, _ = pl.pallas_call(
        block_kernel,
        out_shape=(
            jax.ShapeDtypeStruct((rows // 4, 4 * out_cols), jnp.bfloat16),
            jax.ShapeDtypeStruct((tokens, 4 * cols), jnp.bfloat16),
            jax.ShapeDtypeStruct((4 * o_depth, out_cols), jnp.bfloat16),
        ),
        in_specs=[any_space] * 4,
        out_specs=(any_space,) * 3,
        scratch_shapes=[
            pltpu.VMEM((2, longest, 4 * cols), jnp.bfloat16),
            pltpu.VMEM((4 * max(depth, o_depth), group), jnp.bfloat16),
            pltpu.VMEM((tokens, group), jnp.bfloat16),
            pltpu.VMEM((rows, 4 * o_depth), jnp.bfloat16),
            pltpu.VMEM((4, rows, width), jnp.bfloat16),
            pltpu.VMEM((rows, max(cols, out_cols)), jnp.bfloat16),
            pltpu.VMEM((4,) + seg.shape, jnp.int32),
            pltpu.VMEM((tokens, HEAD_DIM), jnp.int32),
            pltpu.VMEM((1, tokens), jnp.int32),
            dma(7),
            dma(3), dma(3),
            dma(PIECES), dma(PIECES), dma(items, 2, 3), dma(items, 2, 3), dma(items + FIRST), dma(items + FIRST),
            dma(chunks), dma(chunks), dma(chunks), dma(6), dma(2), dma(2),
            dma(9), dma(9), dma(12, 2, 3), dma(12, 2, 3),
            dma(2 * TILES), dma(2 * TILES), dma(2 * TILES), dma(2 * TILES), dma(TILES + 1), dma(TILES + 1), dma(TILES),
            dma(3), dma(3),
        ],
        compiler_params=pltpu.CompilerParams(collective_id=0, has_side_effects=True, vmem_limit_bytes=VMEM_LIMIT),
        name="attention_block",
    )(x, seg, w, wo)
    return y


def solution(mesh):
    shape = dict(mesh.shape)
    assert shape == {"dp": 2, "tp": 4, "sp": 4}

    def device_block(x_block, doc_block, wqkv_block, wout_block):
        return attention_block(x_block, doc_block.reshape(-1, HEAD_DIM), wqkv_block, wout_block)

    return jax.shard_map(
        device_block,
        mesh=mesh,
        in_specs=(P(("dp", "sp"), "tp"), P(("dp", "sp")), P("sp", "tp"), P("sp", "tp")),
        out_specs=P(("dp", "sp", "tp"), None),
        check_vma=False,
    )
```

time: 1370 us -> 500 us (0.36)
  waiting for transfers between devices: 1070 us -> 0 us
  Pallas kernels: 0 us -> 496 us
  matrix products: 139 us -> 0 us
  other arithmetic: 69.3 us -> 0 us
  blocking collectives: 60.5 us -> 0 us
  local copies, waits for them, and re-layouts: 20.9 us -> 3.1 us
    all_gather x5 -> x0, waiting for transfers between devices: 1070 us -> none  [the longest x1 583 us: device_block(): wqkv_cols = lax.all_gather(wqkv_block, 'sp', axis=0, tiled=True)]
    pallas_call x0 -> x1, Pallas kernels: none -> 496 us  [attention_block(): pl.pallas_call(block_kernel, out_shape=(jax.ShapeDtypeStruct((rows // 4,...]
    dot_general x4 -> x0, matrix products: 139 us -> none  [the longest x1 61.2 us: device_block(): jnp.dot(x_rows, wqkv_cols, preferred_element_type=jnp.float32)]
    sub x1 -> x0, other arithmetic: 68.7 us -> none  [device_block(): weights = jax.nn.softmax(scores, axis=-1).astype(jnp.bfloat16)]
    all_to_all x1 -> x0, blocking collectives: 55.3 us -> none  [device_block(): return lax.all_to_all(y_block, 'tp', 0, 1, tiled=True)]
  transfers between devices with their start and end apart: 5 -> 0, of which waited for: 5 -> 0; matrix products, arithmetic and copies ran while one was open for 9% -> 0% of each run, Pallas kernels for 0% -> 0%
where the time goes in v3:
time: 500 us; the launch traced here: 499 us
  Pallas kernels  496 us (99%)
    pallas_call x1, Pallas kernels, attention_block(): pl.pallas_call(block_kernel, out_shape=(jax.ShapeDtypeStruct((rows // 4,...  496 us

profile of v3, /device:TPU:0, one launch (start us, length us, event | category | flops | bytes accessed | tf_op | source)
XLA Modules:
  0.0 499.5 jit_solution(5188115690729865617)
XLA Ops:
  0.0 496.4 %attention_block.1 = (bf16[128,8192]{1,0:T(8,128)(2,1)}, bf16[2048,8192]{1,0:T(8,128)(2,1)}, bf16[8192,2048]{1,0:T(8,128)(2,1)}) custom-call(bf16[512,2048]{1,0:T(8,128)(2,1)} %x_ref.1, s32[4,128]{1,0:T(4,128)} %bitcast.1, bf16[2048,6144]{1,0:T(8,128)(2,1)} %w_ref.1, bf16[2048,2048]{1,0:T(8,128)(2,1)} %wo_ref.1), custom_call_target="tpu_custom_call" | custom-call | tf_op jit(solution)/shard_map/attention_block/pallas_call | solution.py:598
  496.4 3.1 copy.6
